TPU v7x, 32 devices: a whole 2x2x4 slice. The times are simulated.
32 devices in a mesh: sub: 2 (over y), row: 4 (over x, core), col: 4 (over z).
Axes of the slice: x: 2, y: 2, z: 4, core: 2. Of those that a mesh axis runs over, the one named last changes fastest.
Arguments:
- visibility: bfloat16 [2, 16, 512, 4096], P(None, 'sub', 'row', 'col'), may hold values from -13 to 13
- sky_model: bfloat16 [2, 16, 512, 4096], P(None, 'sub', 'row', 'col'), may hold values from -4 to 4, as said below
- antenna_flags: int32 [2, 512], P('sub'), may hold values 0 or 1
- gains_init: float32 [2, 16, 512], P(None, 'sub'), may hold values from -0.5 to 1.5
Outputs:
- gains: float32 [2, 16, 512], P(None, 'sub')
Inputs may be any that keep to these rules, and one draw needn't show every extreme that they name: `sky_model`: model visibility parts lie between -4 and 4.
All inputs are finite; a program needn't handle non-finite values.
Results may differ from a plain program's by a relative error of at most 0.0003.
Values sent between devices are 32-bit elements.
A program may use at most 64 MiB of HBM per device.

v0:
```python
import jax
import jax.numpy as jnp
from jax import lax
from jax.sharding import PartitionSpec as P

TIMES = 8
ITERS = 3


def subband_total(values):
    return lax.psum(values, "sub")


def update_gains(summed, previous):
    denominator = summed[:, 2, :] + 1.0
    quotient = jnp.stack([summed[:, 0, :] / denominator, summed[:, 1, :] / denominator], axis=0)
    updated = 0.5 * (quotient + previous)
    chan_mean = jnp.sum(updated, axis=1) / updated.shape[1]
    overall = subband_total(chan_mean) / lax.axis_size("sub")
    return updated + 0.5 * (overall - chan_mean)[:, None, :]


def time_total(values, selector):
    return jnp.einsum(
        "crk,kq->crq",
        values,
        selector,
        precision=lax.Precision.HIGHEST,
        preferred_element_type=jnp.float32,
    )


def contract(matrix, vector):
    return jnp.einsum("cpq,cq->cp", matrix, vector, precision=lax.Precision.HIGHEST)


def body(visibility, sky_model, antenna_flags, gains_init):
    block_rows = visibility.shape[2]
    wide_cols = visibility.shape[3]
    block_cols = wide_cols // TIMES
    row_at = lax.axis_index("row") * block_rows
    col_at = lax.axis_index("col") * block_cols
    flag_value = antenna_flags[0].astype(jnp.float32)
    row_flag = lax.dynamic_slice_in_dim(flag_value, row_at, block_rows)
    col_flag = lax.dynamic_slice_in_dim(flag_value, col_at, block_cols)
    row_ids = row_at + lax.iota(jnp.int32, block_rows)
    col_ids = col_at + lax.iota(jnp.int32, block_cols)
    weight = (
        row_flag[:, None]
        * col_flag[None, :]
        * (row_ids[:, None] != col_ids[None, :]).astype(jnp.float32)
    )
    selector = (
        lax.iota(jnp.int32, wide_cols)[:, None] // TIMES == lax.iota(jnp.int32, block_cols)[None, :]
    ).astype(jnp.float32)
    vis_re = visibility[0].astype(jnp.float32)
    vis_im = visibility[1].astype(jnp.float32)
    mod_re = sky_model[0].astype(jnp.float32)
    mod_im = sky_model[1].astype(jnp.float32)
    cross_re = time_total(vis_re * mod_re + vis_im * mod_im, selector) * weight
    cross_im = time_total(vis_im * mod_re - vis_re * mod_im, selector) * weight
    power_sum = time_total(mod_re * mod_re + mod_im * mod_im, selector) * weight
    gain_values = gains_init
    for step_index in range(ITERS):
        col_gains = lax.dynamic_slice_in_dim(gain_values, col_at, block_cols, 2)
        gain_re = col_gains[0]
        gain_im = col_gains[1]
        num_re = contract(cross_re, gain_re) - contract(cross_im, gain_im)
        num_im = contract(cross_re, gain_im) + contract(cross_im, gain_re)
        denominator = contract(power_sum, gain_re * gain_re + gain_im * gain_im)
        partial_value = jnp.stack([num_re, num_im, denominator], axis=1)
        summed = lax.psum(partial_value, "col")
        previous = lax.dynamic_slice_in_dim(gain_values, row_at, block_rows, 2)
        gain_block = update_gains(summed, previous)
        gain_values = lax.all_gather(gain_block, "row", axis=2, tiled=True)
    return gain_values


def solution(mesh):
    return jax.shard_map(
        body,
        mesh=mesh,
        in_specs=(
            P(None, "sub", "row", "col"),
            P(None, "sub", "row", "col"),
            P("sub", None),
            P(None, "sub", None),
        ),
        out_specs=P(None, "sub", None),
        check_vma=False,
    )
```

profile of v0, /device:TPU:0, one launch (start us, length us, event | category | flops | bytes accessed | tf_op | source)
XLA Modules:
  0.0 111.2 jit_solution(4182115625880762958)
XLA Ops:
  1.5 6.6 %fusion.25 = f32[8,128,128]{2,1,0:T(8,128)S(1)} fusion(bf16[2,8,128,1024]{3,2,1,0:T(8,128)(2,1)} %param.4, bf16[2,8,128,1024]{3,2,1,0:T(8,128)(2,1)} %param.5, f32[128,128]{1,0:T(8,128)S(1)} %multiply_select_fusion, s32[1024]{0:T(1024)S(1)} %add_select_fusion), kind=kOutput, calls=%fused_computation.26 | convolution fusion | flops 1618214912 | bytes 8982528 | tf_op jit(solution)/shard_map/crk,kq->crq/dot_general | solution.py:24
  8.1 0.9 fusion.61
  9.0 0.9 fusion.59
  10.0 3.0 %fusion.28 = f32[8,128,128]{2,1,0:T(8,128)S(1)} fusion(bf16[2,8,128,1024]{3,2,1,0:T(8,128)(2,1)S(1)} %copy-done.1, bf16[2,8,128,1024]{3,2,1,0:T(8,128)(2,1)S(1)} %copy-done.2, f32[128,128]{1,0:T(8,128)S(1)} %multiply_select_fusion, s32[1024]{0:T(1024)S(1)} %add_select_fusion), kind=kOutput, calls=%fused_computation.27 | convolution fusion | flops 1618214912 | bytes 8982528 | tf_op jit(solution)/shard_map/crk,kq->crq/dot_general | solution.py:24
  13.9 0.9 fusion.58
  14.8 2.7 %fusion.22 = f32[8,128,128]{2,1,0:T(8,128)S(1)} fusion(bf16[2,8,128,1024]{3,2,1,0:T(8,128)(2,1)S(1)} %copy-done.2, f32[128,128]{1,0:T(8,128)S(1)} %multiply_select_fusion, s32[1024]{0:T(1024)S(1)} %add_select_fusion), kind=kOutput, calls=%fused_computation.25 | convolution fusion | flops 1616117760 | bytes 4788224 | tf_op jit(solution)/shard_map/crk,kq->crq/dot_general | solution.py:24
  17.5 0.9 fusion.62
  18.4 20.4 %psum.42 = f32[8,3,128]{2,0,1:T(8,128)S(1)} all-reduce(f32[8,3,128]{2,0,1:T(8,128)S(1)} %pad_maximum_fusion), channel_id=1, replica_groups=mesh['sub'=2,'row'=4,'col'=4] {'col'}, use_global_device_ids=true, to_apply=%region_0.1 | all-reduce | flops 3072 | bytes 24576 | tf_op jit(solution)/shard_map/psum | solution.py:72
  38.9 4.9 %psum.43 = f32[2,128]{1,0:T(2,128)S(1)} all-reduce(f32[2,128]{1,0:T(2,128)S(1)} %broadcast_multiply_fusion.2), channel_id=1, replica_groups=mesh['sub'=2,'row'=4,'col'=4] {'sub'}, use_global_device_ids=true, to_apply=%region_2.3 | all-reduce | flops 256 | bytes 2048 | tf_op jit(solution)/shard_map/psum | solution.py:11
  43.9 5.2 %all_gather.9 = f32[2,8,512]{2,1,0:T(8,128)S(1)} all-gather(f32[2,8,128]{2,1,0:T(8,128)S(1)} %broadcast_add_fusion.2), channel_id=1, replica_groups=mesh['sub'=2,'row'=4,'col'=4] {'row'}, dimensions={2}, use_global_device_ids=true | all-gather | bytes 40960 | tf_op jit(solution)/shard_map/all_gather | solution.py:75
  50.0 0.9 fusion.66
  50.9 0.9 fusion.63
  51.8 0.9 fusion.65
  52.8 0.9 fusion.64
  53.7 15.5 %psum.44 = f32[8,3,128]{2,0,1:T(8,128)S(1)} all-reduce(f32[8,3,128]{2,0,1:T(8,128)S(1)} %pad_maximum_fusion.1), channel_id=1, replica_groups=mesh['sub'=2,'row'=4,'col'=4] {'col'}, use_global_device_ids=true, to_apply=%region_3.4 | all-reduce | flops 3072 | bytes 24576 | tf_op jit(solution)/shard_map/psum | solution.py:72
  69.3 4.9 %psum.45 = f32[2,128]{1,0:T(2,128)S(1)} all-reduce(f32[2,128]{1,0:T(2,128)S(1)} %broadcast_multiply_fusion.1), channel_id=1, replica_groups=mesh['sub'=2,'row'=4,'col'=4] {'sub'}, use_global_device_ids=true, to_apply=%region_5.6 | all-reduce | flops 256 | bytes 2048 | tf_op jit(solution)/shard_map/psum | solution.py:11
  74.3 5.2 %all_gather.10 = f32[2,8,512]{2,1,0:T(8,128)S(1)} all-gather(f32[2,8,128]{2,1,0:T(8,128)S(1)} %broadcast_add_fusion.1), channel_id=1, replica_groups=mesh['sub'=2,'row'=4,'col'=4] {'row'}, dimensions={2}, use_global_device_ids=true | all-gather | bytes 40960 | tf_op jit(solution)/shard_map/all_gather | solution.py:75
  80.4 0.9 fusion.71
  81.3 0.9 fusion.69
  82.2 0.9 fusion.70
  83.2 0.9 fusion.68
  84.1 16.2 %psum.46 = f32[8,3,128]{2,0,1:T(8,128)S(1)} all-reduce(f32[8,3,128]{2,0,1:T(8,128)S(1)} %pad_maximum_fusion.2), channel_id=1, replica_groups=mesh['sub'=2,'row'=4,'col'=4] {'col'}, use_global_device_ids=true, to_apply=%region_6.7 | all-reduce | flops 3072 | bytes 24576 | tf_op jit(solution)/shard_map/psum | solution.py:72
  100.4 4.9 %psum.47 = f32[2,128]{1,0:T(2,128)S(1)} all-reduce(f32[2,128]{1,0:T(2,128)S(1)} %broadcast_multiply_fusion), channel_id=1, replica_groups=mesh['sub'=2,'row'=4,'col'=4] {'sub'}, use_global_device_ids=true, to_apply=%region_8.9 | all-reduce | flops 256 | bytes 2048 | tf_op jit(solution)/shard_map/psum | solution.py:11
  105.3 5.2 %all_gather.11 = f32[2,8,512]{2,1,0:T(8,128)S(1)} all-gather(f32[2,8,128]{2,1,0:T(8,128)S(1)} %broadcast_add_fusion), channel_id=1, replica_groups=mesh['sub'=2,'row'=4,'col'=4] {'row'}, dimensions={2}, use_global_device_ids=true | all-gather | bytes 40960 | tf_op jit(solution)/shard_map/all_gather | solution.py:75
  (42 shorter events, 5.1 us)
Async XLA Ops:
  1.5 8.4 %copy-start.1 = (bf16[2,8,128,1024]{3,2,1,0:T(8,128)(2,1)S(1)}, bf16[2,8,128,1024]{3,2,1,0:T(8,128)(2,1)}, u32[]{:S(2)}) copy-start(bf16[2,8,128,1024]{3,2,1,0:T(8,128)(2,1)} %param.4) | copy-start | bytes 12582916
  1.5 8.4 %copy-start.2 = (bf16[2,8,128,1024]{3,2,1,0:T(8,128)(2,1)S(1)}, bf16[2,8,128,1024]{3,2,1,0:T(8,128)(2,1)}, u32[]{:S(2)}) copy-start(bf16[2,8,128,1024]{3,2,1,0:T(8,128)(2,1)} %param.5) | copy-start | bytes 12582916
  13.9 25.0 %copy-start = (f32[2,8,512]{2,1,0:T(8,128)S(1)}, f32[2,8,512]{2,1,0:T(8,128)}, u32[]{:S(2)}) copy-start(f32[2,8,512]{2,1,0:T(8,128)} %param.7) | copy-start | bytes 98308
where the time goes:
time: 112 us; the launch traced here: 111 us
  blocking collectives  82.5 us (74%)
  matrix products  26.1 us (23%)
  other arithmetic  1.73 us (2%)
    psum x3, blocking collectives, body(): summed = lax.psum(partial_value, 'col')  52.2 us
    all_gather x3, blocking collectives, body(): gain_values = lax.all_gather(gain_block, 'row', axis=2, tiled=True)  15.6 us
    psum x3, blocking collectives, subband_total(): return lax.psum(values, 'sub')  14.8 us
    dot_general x15, matrix products, contract(): jnp.einsum('cpq,cq->cp', matrix, vector, precision=lax.Precision.HIGHEST)  13.9 us
    dot_general x3, matrix products, time_total(): jnp.einsum('crk,kq->crq', values, selector, precision=lax.Precision.HIGHE...  12.3 us

commit v1 on v0

--- a/solution.py
+++ b/solution.py
@@ -69,7 +69,7 @@
         num_im = contract(cross_re, gain_im) + contract(cross_im, gain_re)
         denominator = contract(power_sum, gain_re * gain_re + gain_im * gain_im)
         partial_value = jnp.stack([num_re, num_im, denominator], axis=1)
-        summed = lax.psum(partial_value, "col")
+        summed = jnp.sum(lax.all_gather(partial_value, "col"), axis=0)
         previous = lax.dynamic_slice_in_dim(gain_values, row_at, block_rows, 2)
         gain_block = update_gains(summed, previous)
         gain_values = lax.all_gather(gain_block, "row", axis=2, tiled=True)

time: 112 us -> 100 us (0.89)
  blocking collectives: 82.5 us -> 71.5 us
    psum x3 -> x0, blocking collectives: 52.2 us -> none  [body(): summed = lax.psum(partial_value, 'col')]
    all_gather x0 -> x3, blocking collectives: none -> 40.9 us  [body(): summed = jnp.sum(lax.all_gather(partial_value, 'col'), axis=0)]
where the time goes in v1:
time: 100 us
  blocking collectives  71.5 us (72%)
  matrix products  26.1 us (26%)
  other arithmetic  1.76 us (2%)
    all_gather x3, blocking collectives, body(): summed = jnp.sum(lax.all_gather(partial_value, 'col'), axis=0)  40.9 us
    all_gather x3, blocking collectives, body(): gain_values = lax.all_gather(gain_block, 'row', axis=2, tiled=True)  15.6 us
    psum x3, blocking collectives, subband_total(): return lax.psum(values, 'sub')  15 us
    dot_general x15, matrix products, contract(): jnp.einsum('cpq,cq->cp', matrix, vector, precision=lax.Precision.HIGHEST)  13.9 us
    dot_general x3, matrix products, time_total(): jnp.einsum('crk,kq->crq', values, selector, precision=lax.Precision.HIGHE...  12.3 us

profile of v1, /device:TPU:0, one launch (start us, length us, event | category | flops | bytes accessed | tf_op | source)
XLA Modules:
  0.0 100.1 jit_solution(1204330458822717510)
XLA Ops:
  1.5 6.6 %fusion.25 = f32[8,128,128]{2,1,0:T(8,128)S(1)} fusion(bf16[2,8,128,1024]{3,2,1,0:T(8,128)(2,1)} %param.4, bf16[2,8,128,1024]{3,2,1,0:T(8,128)(2,1)} %param.5, f32[128,128]{1,0:T(8,128)S(1)} %multiply_select_fusion, s32[1024]{0:T(1024)S(1)} %add_select_fusion), kind=kOutput, calls=%fused_computation.26 | convolution fusion | flops 1618214912 | bytes 8982528 | tf_op jit(solution)/shard_map/crk,kq->crq/dot_general | solution.py:24
  8.1 0.9 fusion.61
  9.0 0.9 fusion.59
  10.0 3.0 %fusion.28 = f32[8,128,128]{2,1,0:T(8,128)S(1)} fusion(bf16[2,8,128,1024]{3,2,1,0:T(8,128)(2,1)S(1)} %copy-done.1, bf16[2,8,128,1024]{3,2,1,0:T(8,128)(2,1)S(1)} %copy-done.2, f32[128,128]{1,0:T(8,128)S(1)} %multiply_select_fusion, s32[1024]{0:T(1024)S(1)} %add_select_fusion), kind=kOutput, calls=%fused_computation.27 | convolution fusion | flops 1618214912 | bytes 8982528 | tf_op jit(solution)/shard_map/crk,kq->crq/dot_general | solution.py:24
  13.9 0.9 fusion.58
  14.8 2.7 %fusion.22 = f32[8,128,128]{2,1,0:T(8,128)S(1)} fusion(bf16[2,8,128,1024]{3,2,1,0:T(8,128)(2,1)S(1)} %copy-done.2, f32[128,128]{1,0:T(8,128)S(1)} %multiply_select_fusion, s32[1024]{0:T(1024)S(1)} %add_select_fusion), kind=kOutput, calls=%fused_computation.25 | convolution fusion | flops 1616117760 | bytes 4788224 | tf_op jit(solution)/shard_map/crk,kq->crq/dot_general | solution.py:24
  17.5 0.9 fusion.62
  18.4 14.8 %all-gather = f32[32,3,128]{2,0,1:T(8,128)S(1)} all-gather(f32[8,3,128]{2,0,1:T(8,128)S(1)} %pad_maximum_fusion), channel_id=2, replica_groups=mesh['sub'=2,'row'=4,'col'=4] {'col'}, dimensions={0}, use_global_device_ids=true | all-gather | bytes 61440 | tf_op jit(solution)/shard_map/all_gather | solution.py:72
  33.3 5.1 %psum.21 = f32[2,128]{1,0:T(2,128)S(1)} all-reduce(f32[2,128]{1,0:T(2,128)S(1)} %broadcast_multiply_fusion.2), channel_id=1, replica_groups=mesh['sub'=2,'row'=4,'col'=4] {'sub'}, use_global_device_ids=true, to_apply=%region_2.3 | all-reduce | flops 256 | bytes 2048 | tf_op jit(solution)/shard_map/psum | solution.py:11
  38.4 5.2 %all_gather.29 = f32[2,8,512]{2,1,0:T(8,128)S(1)} all-gather(f32[2,8,128]{2,1,0:T(8,128)S(1)} %broadcast_add_fusion.2), channel_id=1, replica_groups=mesh['sub'=2,'row'=4,'col'=4] {'row'}, dimensions={2}, use_global_device_ids=true | all-gather | bytes 40960 | tf_op jit(solution)/shard_map/all_gather | solution.py:75
  44.5 0.9 fusion.66
  45.4 0.9 fusion.63
  46.4 0.9 fusion.65
  47.3 0.9 fusion.64
  48.3 13.1 %all-gather.1 = f32[32,3,128]{2,0,1:T(8,128)S(1)} all-gather(f32[8,3,128]{2,0,1:T(8,128)S(1)} %pad_maximum_fusion.1), channel_id=3, replica_groups=mesh['sub'=2,'row'=4,'col'=4] {'col'}, dimensions={0}, use_global_device_ids=true | all-gather | bytes 61440 | tf_op jit(solution)/shard_map/all_gather | solution.py:72
  61.4 4.9 %psum.22 = f32[2,128]{1,0:T(2,128)S(1)} all-reduce(f32[2,128]{1,0:T(2,128)S(1)} %broadcast_multiply_fusion.1), channel_id=1, replica_groups=mesh['sub'=2,'row'=4,'col'=4] {'sub'}, use_global_device_ids=true, to_apply=%region_5.6 | all-reduce | flops 256 | bytes 2048 | tf_op jit(solution)/shard_map/psum | solution.py:11
  66.4 5.2 %all_gather.32 = f32[2,8,512]{2,1,0:T(8,128)S(1)} all-gather(f32[2,8,128]{2,1,0:T(8,128)S(1)} %broadcast_add_fusion.1), channel_id=1, replica_groups=mesh['sub'=2,'row'=4,'col'=4] {'row'}, dimensions={2}, use_global_device_ids=true | all-gather | bytes 40960 | tf_op jit(solution)/shard_map/all_gather | solution.py:75
  72.5 0.9 fusion.71
  73.4 0.9 fusion.69
  74.3 0.9 fusion.70
  75.3 0.9 fusion.68
  76.2 13.1 %all-gather.2 = f32[32,3,128]{2,0,1:T(8,128)S(1)} all-gather(f32[8,3,128]{2,0,1:T(8,128)S(1)} %pad_maximum_fusion.2), channel_id=4, replica_groups=mesh['sub'=2,'row'=4,'col'=4] {'col'}, dimensions={0}, use_global_device_ids=true | all-gather | bytes 61440 | tf_op jit(solution)/shard_map/all_gather | solution.py:72
  89.3 4.9 %psum.23 = f32[2,128]{1,0:T(2,128)S(1)} all-reduce(f32[2,128]{1,0:T(2,128)S(1)} %broadcast_multiply_fusion), channel_id=1, replica_groups=mesh['sub'=2,'row'=4,'col'=4] {'sub'}, use_global_device_ids=true, to_apply=%region_8.9 | all-reduce | flops 256 | bytes 2048 | tf_op jit(solution)/shard_map/psum | solution.py:11
  94.3 5.2 %all_gather.35 = f32[2,8,512]{2,1,0:T(8,128)S(1)} all-gather(f32[2,8,128]{2,1,0:T(8,128)S(1)} %broadcast_add_fusion), channel_id=1, replica_groups=mesh['sub'=2,'row'=4,'col'=4] {'row'}, dimensions={2}, use_global_device_ids=true | all-gather | bytes 40960 | tf_op jit(solution)/shard_map/all_gather | solution.py:75
  (45 shorter events, 5.1 us)
Async XLA Ops:
  1.5 8.4 %copy-start.1 = (bf16[2,8,128,1024]{3,2,1,0:T(8,128)(2,1)S(1)}, bf16[2,8,128,1024]{3,2,1,0:T(8,128)(2,1)}, u32[]{:S(2)}) copy-start(bf16[2,8,128,1024]{3,2,1,0:T(8,128)(2,1)} %param.4) | copy-start | bytes 12582916
  1.5 8.4 %copy-start.2 = (bf16[2,8,128,1024]{3,2,1,0:T(8,128)(2,1)S(1)}, bf16[2,8,128,1024]{3,2,1,0:T(8,128)(2,1)}, u32[]{:S(2)}) copy-start(bf16[2,8,128,1024]{3,2,1,0:T(8,128)(2,1)} %param.5) | copy-start | bytes 12582916
  13.9 19.4 %copy-start = (f32[2,8,512]{2,1,0:T(8,128)S(1)}, f32[2,8,512]{2,1,0:T(8,128)}, u32[]{:S(2)}) copy-start(f32[2,8,512]{2,1,0:T(8,128)} %param.7) | copy-start | bytes 98308
